TPU v7x, 32 devices: a whole 2x2x4 slice. The times are simulated.
32 devices in a mesh: dp: 4 (over x, y), tp: 8 (over z, core).
Axes of the slice: x: 2, y: 2, z: 4, core: 2. Of those that a mesh axis runs over, the one named last changes fastest.
Arguments:
- x: bfloat16 [8192, 8192], P('dp'), parts along dimension 0
- w_gate: bfloat16 [8192, 32768], P(None, 'tp')
- w_up: bfloat16 [8192, 32768], P(None, 'tp')
- w_down: bfloat16 [32768, 8192], P('tp')
Outputs:
- output: bfloat16 [8192, 8192], P('dp'), parts along dimension 0
There are 4 independent parts. A program takes and returns all parts, laid end to end along the dimension named above; an argument that names none is the same for every part.
All inputs are finite; a program needn't handle non-finite values.
Results may differ from a plain program's by a relative error of at most 0.016.
Values are sent between devices in bfloat16 or wider.
A program may use at most 2 GiB of HBM per device.

v0:
```python
import jax
import jax.numpy as jnp
from jax import lax
from jax.sharding import PartitionSpec as P


def solution(mesh):
    def step(x, w_gate, w_up, w_down):
        gate = jnp.dot(x, w_gate, preferred_element_type=jnp.float32)
        up = jnp.dot(x, w_up, preferred_element_type=jnp.float32)
        hidden = (jax.nn.silu(gate) * up).astype(jnp.bfloat16)
        term = jnp.dot(hidden, w_down, preferred_element_type=jnp.float32).astype(jnp.bfloat16)
        return lax.psum(term, "tp")

    return jax.shard_map(
        step,
        mesh=mesh,
        in_specs=(P("dp", None), P(None, "tp"), P(None, "tp"), P("tp", None)),
        out_specs=P("dp", None),
        check_vma=False,
    )
```

profile of v0, /device:TPU:0, one launch (start us, length us, event | category | flops | bytes accessed | tf_op | source)
XLA Modules:
  0.0 1151.1 jit_solution(9341621756722852702)
XLA Ops:
  6.5 0.0 all-reduce.2.cloned.1.call-start
  6.5 152.0 %fusion = f32[2048,4096]{1,0:T(8,128)} fusion(bf16[2048,8192]{1,0:T(8,128)(2,1)} %param.4, bf16[8192,4096]{1,0:T(8,128)(2,1)} %param.5), kind=kOutput, calls=%fused_computation.2 | convolution fusion | flops 137438953472 | bytes 134217728 | tf_op jit(solution)/shard_map/dot_general | solution.py:9
  158.6 160.3 %multiply_convert_fusion = bf16[2048,4096]{1,0:T(8,128)(2,1)} fusion(f32[2048,4096]{1,0:T(8,128)} %fusion, bf16[2048,8192]{1,0:T(8,128)(2,1)} %param.4, bf16[8192,4096]{1,0:T(8,128)(2,1)} %param.6), kind=kOutput, calls=%fused_computation | convolution fusion | flops 137489285120 | bytes 150994944 | tf_op jit(solution)/shard_map/dot_general | solution.py:10
  318.8 151.2 %convolution_convert_fusion = bf16[2048,8192]{1,0:T(8,128)(2,1)} fusion(bf16[2048,4096]{1,0:T(8,128)(2,1)} %multiply_convert_fusion, bf16[4096,8192]{1,0:T(8,128)(2,1)} %param.7), kind=kOutput, calls=%fused_computation.1 | convolution fusion | flops 137455730688 | bytes 117440512 | tf_op jit(solution)/shard_map/dot_general | solution.py:12
  470.0 0.0 all-reduce.2.cloned.1.call-update
  470.1 651.2 %all-reduce.2.cloned.1.call-done = bf16[2048,8192]{1,0:T(8,128)(2,1)} async-done(((bf16[2048,8192]{1,0:T(8,128)(2,1)}), bf16[2048,8192]{1,0:T(8,128)(2,1)}) %all-reduce.2.cloned.1.call-update) | async-done | bytes 33554448 | tf_op jit(solution)/shard_map/psum | solution.py:13
  1121.3 23.0 %copy.6 = bf16[2048,8192]{1,0:T(8,128)(2,1)} copy(bf16[2048,8192]{1,0:T(8,128)(2,1)} %all-reduce.2.cloned.1.call-done) | data formatting | bytes 67108864
Async XLA Ops:
  6.5 1114.7 %all-reduce.2.cloned.1.call-start = ((), (), s32[]{:S(2)}) async-start(), calls=%async_computation | async-start | bytes 67108864 | tf_op jit(solution)/shard_map/psum | solution.py:13
Sparse Core Ops, SparseCore 0:
  470.2 651.0 all-reduce.1
where the time goes:
time: 1150 us
  waiting for transfers between devices  651 us (57%)
  matrix products  463 us (40%)
  local copies, waits for them, and re-layouts  23 us (2%)
  between operations  13.4 us (1%)
    psum x1, waiting for transfers between devices, step(): return lax.psum(term, 'tp')  651 us
    dot_general x1, matrix products, step(): up = jnp.dot(x, w_up, preferred_element_type=jnp.float32)  160 us
    dot_general x1, matrix products, step(): gate = jnp.dot(x, w_gate, preferred_element_type=jnp.float32)  152 us
    dot_general x1, matrix products, step(): jnp.dot(hidden, w_down, preferred_element_type=jnp.float32)  151 us
  transfers between devices with their start and end apart: 1, of which 1 were waited for; matrix products, arithmetic and copies ran while one was open for 0% of the time, Pallas kernels for 0%

commit v1 on v0

v1 whole, which is shorter than its diff:
```python
import functools

import jax
import jax.numpy as jnp
from jax import lax
from jax.experimental import pallas as pl
from jax.experimental.pallas import tpu as pltpu
from jax.sharding import PartitionSpec as P

MESH = pl.DeviceIdType.MESH
BF16, F32 = jnp.bfloat16, jnp.float32

T = 256
R = 256
H = R // 2
BIG, SMALL = 512, 256
NBIG, NSMALL = 3, 2
N_OWN, N_PRECV, N_RO, N_RI, N_PS, N_AS, N_FS, N_Y = 17, 14, 14, 12, 4, 8, 8, 24
LAG_P, LAG_AO, LAG_AI, LAG_F, LAG_Y1, LAG_Y2 = 4, 4, 9, 14, 19, 24


def kernel(
    d, f, x, wg, wu, wd, y,
    xb, hid, wgu, wdb, gu, own, precv, ro, ri, ps, asd, fs,
    wsem, xsem, ps_sem, precv_sem, as_sem, ro_sem, ri_sem, fs_sem, ya_sem, yb_sem, yp_sem, fw_sem,
):
    half = d // 2
    steps = f // T
    assert half // T == steps
    n_units = steps * (NBIG * BIG + NSMALL * SMALL) // R
    per_big = BIG // R
    big_units = NBIG * steps * per_big

    tp = lax.axis_index("tp")
    z, c = lax.div(tp, 2), lax.rem(tp, 2)
    inner = jnp.logical_and(z >= 1, z <= 2)
    outer = jnp.logical_not(inner)
    partner = {"tp": z * 2 + 1 - c}
    near = 1 + lax.div(z, 2)
    to_near = {"tp": near * 2 + c}
    to_inner = {"tp": (3 - near) * 2 + c}
    to_outer = {"tp": 3 * (near - 1) * 2 + c}
    near_rows = (near - 1) * H
    far_rows = (2 - near) * H
    my_cols, other_cols = c * half, (1 - c) * half

    def remote(src, dst, send, recv, dev):
        return pltpu.make_async_remote_copy(
            src_ref=src, dst_ref=dst, send_sem=send, recv_sem=recv, device_id=dev, device_id_type=MESH
        )

    def valid(v):
        return jnp.logical_and(v >= 0, v < n_units)

    def slot(v, n):
        return jnp.where(valid(v), lax.rem(v + 64 * n, n), n)

    def unit_at(v):
        b = jnp.where(v < big_units, 1, 0)
        w = v - big_units
        row_b = lax.div(v, steps * per_big) * BIG + lax.rem(v, per_big) * R
        col_b = lax.div(lax.rem(v, steps * per_big), per_big) * T
        row_s = NBIG * BIG + lax.div(w, steps) * SMALL
        col_s = lax.rem(w, steps) * T
        row = b * row_b + (1 - b) * row_s
        col = b * col_b + (1 - b) * col_s
        return row, col

    def y_at(v, rows):
        row, col = unit_at(v)
        return y.at[pl.ds(pl.multiple_of(row + rows, H), H), pl.ds(pl.multiple_of(my_cols + col, T), T)]

    def g_copies(j, s):
        cols = pl.ds(pl.multiple_of(j * T, T), T)
        return [
            pltpu.make_async_copy(wg.at[:, cols], wgu.at[s, :, pl.ds(0, T)], wsem.at[s, 0]),
            pltpu.make_async_copy(wu.at[:, cols], wgu.at[s, :, pl.ds(T, T)], wsem.at[s, 1]),
        ]

    def d_copies(j, s):
        theirs = pl.ds(pl.multiple_of(other_cols + j * T, T), T)
        mine = pl.ds(pl.multiple_of(my_cols + j * T, T), T)
        return [
            pltpu.make_async_copy(wd.at[:, theirs], wdb.at[s, :, pl.ds(0, T)], wsem.at[s, 2]),
            pltpu.make_async_copy(wd.at[:, mine], wdb.at[s, :, pl.ds(T, T)], wsem.at[s, 3]),
        ]

    def x_copy(row, rows, s):
        return pltpu.make_async_copy(x.at[pl.ds(row, rows)], xb.at[s, pl.ds(0, rows)], xsem.at[s])

    def start(copies):
        for cp in copies:
            cp.start()

    def wait(copies):
        for cp in copies:
            cp.wait()

    def ps_copy(v):
        s = lax.rem(v, N_PS)
        return remote(ps.at[s], precv.at[lax.rem(v, N_PRECV)], ps_sem.at[s], precv_sem.at[lax.rem(v, N_PRECV)], partner)

    def ps_free(v):
        @pl.when(v >= N_PS)
        def _():
            ps_copy(v - N_PS).wait_send()

    def p_wait(v):
        @pl.when(valid(v))
        def _():
            ps_copy(v).wait_recv()

    def ao_copy(v):
        s = lax.rem(v, N_AS)
        return remote(asd.at[s], ro.at[lax.rem(v, N_RO)], as_sem.at[s], ro_sem.at[lax.rem(v, N_RO)], to_near)

    def ai_copy(v):
        s = lax.rem(v, N_AS)
        rows = pl.ds(pl.multiple_of(far_rows, H), H)
        return remote(asd.at[s, rows], ri.at[lax.rem(v, N_RI)], as_sem.at[s], ri_sem.at[lax.rem(v, N_RI)], to_inner)

    def a_wait(vo, vi):
        @pl.when(jnp.logical_and(outer, jnp.logical_and(vo >= N_AS, vo < n_units)))
        def _():
            ao_copy(vo - N_AS).wait_send()

        @pl.when(jnp.logical_and(inner, jnp.logical_and(vi >= N_AS, vi < n_units)))
        def _():
            ai_copy(vi - N_AS).wait_send()

        @pl.when(jnp.logical_and(inner, valid(vi)))
        def _():
            ao_copy(vi).wait_recv()

    def a_compute(vo, vi):
        v = jnp.where(inner, vi, vo)
        so = slot(v, N_OWN)
        sr = jnp.where(inner, slot(v, N_RO), N_RO)
        total = own[so] + precv[slot(v, N_PRECV)].astype(F32) + ro[sr].astype(F32)
        own[so] = total
        asd[slot(v, N_AS)] = total.astype(BF16)

    def a_start(vo, vi):
        @pl.when(jnp.logical_and(outer, valid(vo)))
        def _():
            ao_copy(vo).start()

        @pl.when(jnp.logical_and(inner, valid(vi)))
        def _():
            ai_copy(vi).start()

    def f_copies(v):
        s = lax.rem(v, N_FS)
        at = y_at(v, near_rows)
        ys = lax.rem(v, N_Y)
        return [
            remote(fs.at[s], at, fs_sem.at[s, 0], ya_sem.at[ys], to_outer),
            remote(fs.at[s], at, fs_sem.at[s, 1], ya_sem.at[ys], to_inner),
            remote(fs.at[s], at, fs_sem.at[s, 2], yp_sem, partner),
            pltpu.make_async_copy(fs.at[s], at, fs_sem.at[s, 3]),
        ]

    def f_wait_sends(v):
        copies = f_copies(v)
        for cp in copies[:3]:
            cp.wait_send()
        copies[3].wait()

    def f_wait(v):
        @pl.when(jnp.logical_and(inner, jnp.logical_and(v >= N_FS, v < n_units)))
        def _():
            f_wait_sends(v - N_FS)

        @pl.when(jnp.logical_and(inner, valid(v)))
        def _():
            ai_copy(v).wait_recv()

    def f_compute(v):
        v = jnp.where(inner, v, -1)
        rows = pl.ds(pl.multiple_of(near_rows, H), H)
        fs[slot(v, N_FS)] = (own[slot(v, N_OWN), rows, :] + ri[slot(v, N_RI)].astype(F32)).astype(BF16)

    def f_start(v):
        @pl.when(jnp.logical_and(inner, valid(v)))
        def _():
            start(f_copies(v))

    def y1(v):
        @pl.when(jnp.logical_and(inner, valid(v)))
        def _():
            at = y_at(v, far_rows)
            remote(at, at, fw_sem, ya_sem.at[lax.rem(v, N_Y)], to_inner).wait_recv()
            remote(at, at, fw_sem, yb_sem.at[lax.rem(v, N_Y)], to_outer).start()
            remote(at, at, fw_sem, yp_sem, partner).start()

        @pl.when(jnp.logical_and(outer, valid(v)))
        def _():
            at = y_at(v, near_rows)
            remote(at, at, fw_sem, ya_sem.at[lax.rem(v, N_Y)], to_near).wait_recv()
            remote(at, at, fw_sem, yp_sem, partner).start()

    def y2(v):
        @pl.when(jnp.logical_and(outer, valid(v)))
        def _():
            at = y_at(v, far_rows)
            remote(at, at, fw_sem, yb_sem.at[lax.rem(v, N_Y)], to_near).wait_recv()
            remote(at, at, fw_sem, yp_sem, partner).start()

    def waits(u0, r):
        for i in range(r):
            p_wait(u0 - LAG_P + i)
        for i in range(r):
            a_wait(u0 - LAG_AO + i, u0 - LAG_AI + i)
        for i in range(r):
            f_wait(u0 - LAG_F + i)
        for i in range(r):
            y1(u0 - LAG_Y1 + i)
        for i in range(r):
            y2(u0 - LAG_Y2 + i)

    def computes(u0, r):
        for i in range(r):
            a_compute(u0 - LAG_AO + i, u0 - LAG_AI + i)
        for i in range(r):
            f_compute(u0 - LAG_F + i)

    def starts(u0, r):
        for i in range(r):
            a_start(u0 - LAG_AO + i, u0 - LAG_AI + i)
        for i in range(r):
            f_start(u0 - LAG_F + i)

    def epilogue(rows, s, j):
        g, u = gu[pl.ds(0, rows), pl.ds(0, T)], gu[pl.ds(0, rows), pl.ds(T, T)]
        h = (g * jax.nn.sigmoid(g) * u).astype(BF16)
        hid[s, pl.ds(0, rows), pl.ds(pl.multiple_of(j * T, T), T)] = h

    def gate_up(rows, s, w):
        gu[pl.ds(0, rows), :] = jnp.dot(xb[s, pl.ds(0, rows)], wgu[w], preferred_element_type=F32)

    def down(rows, s, w, u0):
        t = jnp.dot(hid[s, pl.ds(0, rows)], wdb[w], preferred_element_type=F32)
        for i in range(rows // R):
            part = t[i * R : (i + 1) * R]
            ps[lax.rem(u0 + i, N_PS)] = part[:, :T].astype(BF16)
            own[lax.rem(u0 + i, N_OWN)] = part[:, T:]

    barrier = pltpu.get_barrier_semaphore()
    x_copy(0, BIG, 0).start()
    start(g_copies(0, 0))
    pl.semaphore_signal(barrier, inc=1, device_id=partner, device_id_type=MESH)

    @pl.when(outer)
    def _():
        pl.semaphore_signal(barrier, inc=1, device_id=to_near, device_id_type=MESH)

    @pl.when(inner)
    def _():
        pl.semaphore_signal(barrier, inc=1, device_id=to_outer, device_id_type=MESH)
        pl.semaphore_signal(barrier, inc=1, device_id=to_inner, device_id_type=MESH)

    gu[...] = jnp.zeros_like(gu)
    ro[N_RO] = jnp.zeros((R, T), BF16)
    x_copy(0, BIG, 0).wait()

    def first(j, _):
        w = lax.rem(j, 2)

        @pl.when(j < steps - 1)
        def _():
            start(g_copies(j + 1, 1 - w))

        @pl.when(j == steps - 1)
        def _():
            start(g_copies(0, 1 - w))
            start(d_copies(0, 1 - w))

        @pl.when(j == 1)
        def _():
            x_copy(BIG, BIG, 1).start()

        wait(g_copies(j, w))
        epilogue(BIG, 0, lax.rem(j + steps - 1, steps))
        gate_up(BIG, 0, w)
        return 0

    lax.fori_loop(0, steps, first, 0)

    @pl.when(outer)
    def _():
        pl.semaphore_wait(barrier, 2)

    @pl.when(inner)
    def _():
        pl.semaphore_wait(barrier, 3)

    def both(t, _):
        k, j = lax.div(t, steps), lax.rem(t, steps)
        w = lax.rem(t, 2)
        sd, sg = lax.rem(k, 2), lax.rem(k + 1, 2)
        u0 = t * per_big
        jn = lax.rem(j + 1, steps)
        start(g_copies(jn, 1 - w))
        start(d_copies(jn, 1 - w))

        @pl.when(j == 0)
        def _():
            x_copy(0, BIG, sg).wait()

        for kk in range(NBIG - 1):
            rows = BIG if kk + 2 < NBIG else SMALL

            @pl.when(t == kk * steps + 1)
            def _():
                x_copy((kk + 2) * BIG, rows, kk % 2).start()

        for i in range(per_big):
            ps_free(u0 + i)
        waits(u0, per_big)
        wait(g_copies(j, w))
        wait(d_copies(j, w))
        epilogue(BIG, jnp.where(j == 0, sd, sg), lax.rem(j + steps - 1, steps))
        computes(u0, per_big)
        gate_up(BIG, sg, w)
        down(BIG, sd, w, u0)
        for i in range(per_big):
            ps_copy(u0 + i).start()
        starts(u0, per_big)
        return 0

    lax.fori_loop(0, steps * (NBIG - 1), both, 0)

    for k in range(NBIG - 1, NBIG + NSMALL - 1):
        rows = BIG if k < NBIG else SMALL
        r = rows // R
        base = (NBIG - 1) * steps * per_big if k < NBIG else big_units + (k - NBIG) * steps
        sd, sg = k % 2, (k + 1) % 2
        last = k == NBIG + NSMALL - 2
        x_copy(0, SMALL, sg).wait()

        def small(j, _, rows=rows, r=r, base=base, sd=sd, sg=sg, last=last, k=k):
            w = lax.rem(j, 2)
            u0 = base + j * r
            jn = lax.rem(j + 1, steps)
            if last:

                @pl.when(j < steps - 1)
                def _():
                    start(g_copies(jn, 1 - w))
            else:
                start(g_copies(jn, 1 - w))
            start(d_copies(jn, 1 - w))
            if not last:

                @pl.when(j == 1)
                def _():
                    x_copy(NBIG * BIG + (k + 2 - NBIG) * SMALL, SMALL, sd).start()

            for i in range(r):
                ps_free(u0 + i)
            waits(u0, r)
            wait(g_copies(j, w))
            wait(d_copies(j, w))
            epilogue(rows, jnp.where(j == 0, sd, sg), lax.rem(j + steps - 1, steps))
            computes(u0, r)
            gate_up(SMALL, sg, w)
            down(rows, sd, w, u0)
            for i in range(r):
                ps_copy(u0 + i).start()
            starts(u0, r)
            return 0

        lax.fori_loop(0, steps, small, 0)

    sd = (NBIG + NSMALL - 1) % 2
    epilogue(SMALL, sd, steps - 1)

    def final(j, _):
        w = lax.rem(j, 2)
        u0 = n_units - steps + j

        @pl.when(j < steps - 1)
        def _():
            start(d_copies(j + 1, 1 - w))

        ps_free(u0)
        waits(u0, 1)
        wait(d_copies(j, w))
        computes(u0, 1)
        down(SMALL, sd, w, u0)
        ps_copy(u0).start()
        starts(u0, 1)
        return 0

    lax.fori_loop(0, steps, final, 0)

    def drain(i, _):
        u0 = n_units + i
        waits(u0, 1)
        computes(u0, 1)
        starts(u0, 1)
        return 0

    lax.fori_loop(0, LAG_Y2, drain, 0)

    for v in range(n_units - N_PS, n_units):
        ps_copy(v).wait_send()

    @pl.when(outer)
    def _():
        for v in range(n_units - N_AS, n_units):
            ao_copy(v).wait_send()

    @pl.when(inner)
    def _():
        for v in range(n_units - N_AS, n_units):
            ai_copy(v).wait_send()
        for v in range(n_units - N_FS, n_units):
            f_wait_sends(v)

    sent = y.at[:, pl.ds(pl.multiple_of(my_cols, T), half)]
    got = y.at[:, pl.ds(pl.multiple_of(other_cols, T), half)]
    remote(sent, got, fw_sem, yp_sem, partner).wait_send()
    remote(sent, got, fw_sem, yp_sem, partner).wait_recv()


def solution(mesh):
    def step(x, w_gate, w_up, w_down):
        d, f = w_gate.shape
        rows = x.shape[0]
        assert rows == NBIG * BIG + NSMALL * SMALL
        dma, vmem = pltpu.SemaphoreType.DMA, pltpu.VMEM
        return pl.pallas_call(
            functools.partial(kernel, d, f),
            out_shape=jax.ShapeDtypeStruct((rows, d), BF16),
            in_specs=[pl.BlockSpec(memory_space=pltpu.HBM)] * 4,
            out_specs=pl.BlockSpec(memory_space=pltpu.HBM),
            scratch_shapes=[
                vmem((2, BIG, d), BF16),
                vmem((2, BIG, f), BF16),
                vmem((2, d, 2 * T), BF16),
                vmem((2, f, 2 * T), BF16),
                vmem((BIG, 2 * T), F32),
                vmem((N_OWN + 1, R, T), F32),
                vmem((N_PRECV + 1, R, T), BF16),
                vmem((N_RO + 1, R, T), BF16),
                vmem((N_RI + 1, H, T), BF16),
                vmem((N_PS, R, T), BF16),
                vmem((N_AS + 1, R, T), BF16),
                vmem((N_FS + 1, H, T), BF16),
                dma((2, 4)),
                dma((2,)),
                dma((N_PS,)),
                dma((N_PRECV,)),
                dma((N_AS,)),
                dma((N_RO,)),
                dma((N_RI,)),
                dma((N_FS, 4)),
                dma((N_Y,)),
                dma((N_Y,)),
                dma,
                dma,
            ],
            compiler_params=pltpu.CompilerParams(
                collective_id=0, has_side_effects=True, vmem_limit_bytes=67043328
            ),
            name="mlp",
        )(x, w_gate, w_up, w_down)

    return jax.shard_map(
        step,
        mesh=mesh,
        in_specs=(P("dp", None), P(None, "tp"), P(None, "tp"), P("tp", None)),
        out_specs=P("dp", None),
        check_vma=False,
    )
```

time: 1150 us -> 586 us (0.51)
  waiting for transfers between devices: 651 us -> 0 us
  Pallas kernels: 0 us -> 563 us
  matrix products: 463 us -> 0 us
  between operations: 13.4 us -> 0.01 us
    psum x1 -> x0, waiting for transfers between devices: 651 us -> none  [step(): return lax.psum(term, 'tp')]
    pallas_call x0 -> x1, Pallas kernels: none -> 563 us  [step(): pl.pallas_call(functools.partial(kernel, d, f), out_shape=jax.ShapeDtypeS...]
    dot_general x3 -> x0, matrix products: 463 us -> none  [the longest x1 160 us: step(): up = jnp.dot(x, w_up, preferred_element_type=jnp.float32)]
  transfers between devices with their start and end apart: 1 -> 0, of which waited for: 1 -> 0; matrix products, arithmetic and copies ran while one was open for 0% -> 0% of each run, Pallas kernels for 0% -> 0%
where the time goes in v1:
time: 586 us
  Pallas kernels  563 us (96%)
  local copies, waits for them, and re-layouts  23 us (4%)
    pallas_call x1, Pallas kernels, step(): pl.pallas_call(functools.partial(kernel, d, f), out_shape=jax.ShapeDtypeS...  563 us
    unnamed x1, local copies, waits for them, and re-layouts  23 us

profile of v1, /device:TPU:0, one launch (start us, length us, event | category | flops | bytes accessed | tf_op | source)
XLA Modules:
  0.0 585.9 jit_solution(4130015087371873862)
XLA Ops:
  0.0 562.9 %mlp.1 = bf16[2048,8192]{1,0:T(8,128)(2,1)} custom-call(bf16[2048,8192]{1,0:T(8,128)(2,1)} %x.1, bf16[8192,4096]{1,0:T(8,128)(2,1)} %wg.1, bf16[8192,4096]{1,0:T(8,128)(2,1)} %wu.1, bf16[4096,8192]{1,0:T(8,128)(2,1)} %wd.1), custom_call_target="tpu_custom_call" | custom-call | tf_op jit(solution)/shard_map/mlp/pallas_call | solution.py:433
  562.9 23.0 %copy.6 = bf16[2048,8192]{1,0:T(8,128)(2,1)} copy(bf16[2048,8192]{1,0:T(8,128)(2,1)} %mlp.1) | data formatting | bytes 67108864

commit v2 on v1

--- a/solution.py
+++ b/solution.py
@@ -15,8 +15,10 @@
 H = R // 2
 BIG, SMALL = 512, 256
 NBIG, NSMALL = 3, 2
-N_OWN, N_PRECV, N_RO, N_RI, N_PS, N_AS, N_FS, N_Y = 17, 14, 14, 12, 4, 8, 8, 24
-LAG_P, LAG_AO, LAG_AI, LAG_F, LAG_Y1, LAG_Y2 = 4, 4, 9, 14, 19, 24
+N_OWN, N_PRECV, N_RO, N_RI, N_PS, N_AS, N_FS, N_Y = 13, 10, 11, 11, 4, 8, 8, 14
+FAR = {"p": 2, "ao": 2, "ai": 5, "f": 8, "y1": 12, "y2": 15}
+WIDE = {"p": 2, "ao": 2, "ai": 7, "f": 12, "y1": 17, "y2": 20}
+NEAR = {"p": 2, "ao": 2, "ai": 4, "f": 6, "y1": 8, "y2": 10}
 
 
 def kernel(
@@ -119,35 +121,34 @@
         rows = pl.ds(pl.multiple_of(far_rows, H), H)
         return remote(asd.at[s, rows], ri.at[lax.rem(v, N_RI)], as_sem.at[s], ri_sem.at[lax.rem(v, N_RI)], to_inner)
 
-    def a_wait(vo, vi):
-        @pl.when(jnp.logical_and(outer, jnp.logical_and(vo >= N_AS, vo < n_units)))
-        def _():
-            ao_copy(vo - N_AS).wait_send()
-
-        @pl.when(jnp.logical_and(inner, jnp.logical_and(vi >= N_AS, vi < n_units)))
-        def _():
-            ai_copy(vi - N_AS).wait_send()
-
-        @pl.when(jnp.logical_and(inner, valid(vi)))
-        def _():
-            ao_copy(vi).wait_recv()
-
-    def a_compute(vo, vi):
-        v = jnp.where(inner, vi, vo)
+    def a_wait(v):
+        @pl.when(jnp.logical_and(outer, jnp.logical_and(v >= N_AS, v < n_units)))
+        def _():
+            ao_copy(v - N_AS).wait_send()
+
+        @pl.when(jnp.logical_and(inner, jnp.logical_and(v >= N_AS, v < n_units)))
+        def _():
+            ai_copy(v - N_AS).wait_send()
+
+        @pl.when(jnp.logical_and(inner, valid(v)))
+        def _():
+            ao_copy(v).wait_recv()
+
+    def a_compute(v):
         so = slot(v, N_OWN)
         sr = jnp.where(inner, slot(v, N_RO), N_RO)
         total = own[so] + precv[slot(v, N_PRECV)].astype(F32) + ro[sr].astype(F32)
         own[so] = total
         asd[slot(v, N_AS)] = total.astype(BF16)
 
-    def a_start(vo, vi):
-        @pl.when(jnp.logical_and(outer, valid(vo)))
-        def _():
-            ao_copy(vo).start()
-
-        @pl.when(jnp.logical_and(inner, valid(vi)))
-        def _():
-            ai_copy(vi).start()
+    def a_start(v):
+        @pl.when(jnp.logical_and(outer, valid(v)))
+        def _():
+            ao_copy(v).start()
+
+        @pl.when(jnp.logical_and(inner, valid(v)))
+        def _():
+            ai_copy(v).start()
 
     def f_copies(v):
         s = lax.rem(v, N_FS)
@@ -206,29 +207,61 @@
             remote(at, at, fw_sem, yb_sem.at[lax.rem(v, N_Y)], to_near).wait_recv()
             remote(at, at, fw_sem, yp_sem, partner).start()
 
-    def waits(u0, r):
-        for i in range(r):
-            p_wait(u0 - LAG_P + i)
-        for i in range(r):
-            a_wait(u0 - LAG_AO + i, u0 - LAG_AI + i)
-        for i in range(r):
-            f_wait(u0 - LAG_F + i)
-        for i in range(r):
-            y1(u0 - LAG_Y1 + i)
-        for i in range(r):
-            y2(u0 - LAG_Y2 + i)
-
-    def computes(u0, r):
-        for i in range(r):
-            a_compute(u0 - LAG_AO + i, u0 - LAG_AI + i)
-        for i in range(r):
-            f_compute(u0 - LAG_F + i)
-
-    def starts(u0, r):
-        for i in range(r):
-            a_start(u0 - LAG_AO + i, u0 - LAG_AI + i)
-        for i in range(r):
-            f_start(u0 - LAG_F + i)
+    def stages(at):
+        p_wait(at["p"])
+        a_wait(at["a"])
+
+        @pl.when(valid(at["a"]))
+        def _():
+            a_compute(at["a"])
+
+        a_start(at["a"])
+        f_wait(at["f"])
+
+        @pl.when(jnp.logical_and(inner, valid(at["f"])))
+        def _():
+            f_compute(at["f"])
+
+        f_start(at["f"])
+        y1(at["y1"])
+        y2(at["y2"])
+
+    def waits(ats):
+        for fn, key in ((p_wait, "p"), (a_wait, "a"), (f_wait, "f"), (y1, "y1"), (y2, "y2")):
+            for at in ats:
+                fn(at[key])
+
+    def computes(ats):
+        for at in ats:
+            a_compute(at["a"])
+        for at in ats:
+            f_compute(at["f"])
+
+    def starts(ats):
+        for at in ats:
+            a_start(at["a"])
+        for at in ats:
+            f_start(at["f"])
+
+    def by_role(lags):
+        return {"p": lags["p"], "a": jnp.where(inner, lags["ai"], lags["ao"]), "f": lags["f"], "y1": lags["y1"], "y2": lags["y2"]}
+
+    far, wide, near_end = by_role(FAR), by_role(WIDE), by_role(NEAR)
+
+    def behind(u, lags):
+        return {k: u - v for k, v in lags.items()}
+
+    def opening(base, q):
+        turns = steps * per_big
+        at = {}
+        for k in far:
+            now = q - lax.div(q * (wide[k] - far[k]), turns)
+            then = q + 1 - lax.div((q + 1) * (wide[k] - far[k]), turns)
+            at[k] = jnp.where(then == now, -1, base - far[k] + now)
+        return at
+
+    def closing(base, j):
+        return {k: base - wide[k] + j + lax.div(j * (wide[k] - near_end[k]), steps) for k in wide}
 
     def epilogue(rows, s, j):
         g, u = gu[pl.ds(0, rows), pl.ds(0, T)], gu[pl.ds(0, rows), pl.ds(T, T)]
@@ -244,6 +277,28 @@
             part = t[i * R : (i + 1) * R]
             ps[lax.rem(u0 + i, N_PS)] = part[:, :T].astype(BF16)
             own[lax.rem(u0 + i, N_OWN)] = part[:, T:]
+
+    def two_units(rows, sd, sg, w, j, u0, ats):
+
+        @pl.when(j == 0)
+        def _():
+            epilogue(BIG, sd, steps - 1)
+
+        for i in range(per_big):
+            ps_free(u0 + i)
+        waits(ats[:1])
+        wait(d_copies(j, w))
+        computes(ats[:1])
+        down(BIG, sd, w, u0)
+        for i in range(per_big):
+            ps_copy(u0 + i).start()
+        starts(ats[:1])
+        waits(ats[1:])
+        wait(g_copies(j, w))
+        epilogue(rows, jnp.where(j == 0, sd, sg), lax.rem(j + steps - 1, steps))
+        computes(ats[1:])
+        gate_up(rows, sg, w)
+        starts(ats[1:])
 
     barrier = pltpu.get_barrier_semaphore()
     x_copy(0, BIG, 0).start()
@@ -314,31 +369,19 @@
             def _():
                 x_copy((kk + 2) * BIG, rows, kk % 2).start()
 
-        for i in range(per_big):
-            ps_free(u0 + i)
-        waits(u0, per_big)
-        wait(g_copies(j, w))
-        wait(d_copies(j, w))
-        epilogue(BIG, jnp.where(j == 0, sd, sg), lax.rem(j + steps - 1, steps))
-        computes(u0, per_big)
-        gate_up(BIG, sg, w)
-        down(BIG, sd, w, u0)
-        for i in range(per_big):
-            ps_copy(u0 + i).start()
-        starts(u0, per_big)
+        two_units(BIG, sd, sg, w, j, u0, [behind(u0 + i, far) for i in range(per_big)])
         return 0
 
     lax.fori_loop(0, steps * (NBIG - 1), both, 0)
 
     for k in range(NBIG - 1, NBIG + NSMALL - 1):
-        rows = BIG if k < NBIG else SMALL
-        r = rows // R
+        r = per_big if k < NBIG else 1
         base = (NBIG - 1) * steps * per_big if k < NBIG else big_units + (k - NBIG) * steps
         sd, sg = k % 2, (k + 1) % 2
         last = k == NBIG + NSMALL - 2
         x_copy(0, SMALL, sg).wait()
 
-        def small(j, _, rows=rows, r=r, base=base, sd=sd, sg=sg, last=last, k=k):
+        def small(j, _, r=r, base=base, sd=sd, sg=sg, last=last, k=k):
             w = lax.rem(j, 2)
             u0 = base + j * r
             jn = lax.rem(j + 1, steps)
@@ -356,18 +399,27 @@
                 def _():
                     x_copy(NBIG * BIG + (k + 2 - NBIG) * SMALL, SMALL, sd).start()
 
-            for i in range(r):
-                ps_free(u0 + i)
-            waits(u0, r)
+            if k < NBIG:
+                two_units(SMALL, sd, sg, w, j, u0, [opening(base, j * r + i) for i in range(r)])
+                return 0
+
+            @pl.when(j == 0)
+            def _():
+                epilogue(SMALL, sd, steps - 1)
+
+            one, two = closing(base, j), closing(base, j + 1)
+            stages({a: jnp.where(two[a] - one[a] == 2, one[a], -1) for a in one})
+            ats = [{a: two[a] - 1 for a in two}]
+            ps_free(u0)
+            waits(ats)
+            wait(d_copies(j, w))
+            computes(ats)
+            down(SMALL, sd, w, u0)
+            ps_copy(u0).start()
+            starts(ats)
             wait(g_copies(j, w))
-            wait(d_copies(j, w))
-            epilogue(rows, jnp.where(j == 0, sd, sg), lax.rem(j + steps - 1, steps))
-            computes(u0, r)
+            epilogue(SMALL, jnp.where(j == 0, sd, sg), lax.rem(j + steps - 1, steps))
             gate_up(SMALL, sg, w)
-            down(rows, sd, w, u0)
-            for i in range(r):
-                ps_copy(u0 + i).start()
-            starts(u0, r)
             return 0
 
         lax.fori_loop(0, steps, small, 0)
@@ -383,25 +435,20 @@
         def _():
             start(d_copies(j + 1, 1 - w))
 
+        stages(behind(u0, near_end))
         ps_free(u0)
-        waits(u0, 1)
         wait(d_copies(j, w))
-        computes(u0, 1)
         down(SMALL, sd, w, u0)
         ps_copy(u0).start()
-        starts(u0, 1)
         return 0
 
     lax.fori_loop(0, steps, final, 0)
 
     def drain(i, _):
-        u0 = n_units + i
-        waits(u0, 1)
-        computes(u0, 1)
-        starts(u0, 1)
+        stages(behind(n_units + i, near_end))
         return 0
 
-    lax.fori_loop(0, LAG_Y2, drain, 0)
+    lax.fori_loop(0, NEAR["y2"], drain, 0)
 
     for v in range(n_units - N_PS, n_units):
         ps_copy(v).wait_send()

time: 586 us -> 558 us (0.952)
  Pallas kernels: 563 us -> 535 us
    pallas_call x1, Pallas kernels: 563 us -> 535 us  [step(): pl.pallas_call(functools.partial(kernel, d, f), out_shape=jax.ShapeDtypeS...]
where the time goes in v2:
time: 558 us
  Pallas kernels  535 us (96%)
  local copies, waits for them, and re-layouts  23 us (4%)
    pallas_call x1, Pallas kernels, step(): pl.pallas_call(functools.partial(kernel, d, f), out_shape=jax.ShapeDtypeS...  535 us
    unnamed x1, local copies, waits for them, and re-layouts  23 us

profile of v2, /device:TPU:0, one launch (start us, length us, event | category | flops | bytes accessed | tf_op | source)
XLA Modules:
  0.0 557.7 jit_solution(8213090004018688462)
XLA Ops:
  0.0 534.7 %mlp.1 = bf16[2048,8192]{1,0:T(8,128)(2,1)} custom-call(bf16[2048,8192]{1,0:T(8,128)(2,1)} %x.1, bf16[8192,4096]{1,0:T(8,128)(2,1)} %wg.1, bf16[8192,4096]{1,0:T(8,128)(2,1)} %wu.1, bf16[4096,8192]{1,0:T(8,128)(2,1)} %wd.1), custom_call_target="tpu_custom_call" | custom-call | tf_op jit(solution)/shard_map/mlp/pallas_call | solution.py:480
  534.7 23.0 %copy.6 = bf16[2048,8192]{1,0:T(8,128)(2,1)} copy(bf16[2048,8192]{1,0:T(8,128)(2,1)} %mlp.1) | data formatting | bytes 67108864
